TPU v7x, 1024 devices: a whole 4x4x32 slice. The times are simulated.
1024 devices in a mesh: gx: 128 (over z, y), gy: 8 (over x, core).
Axes of the slice: x: 4, y: 4, z: 32, core: 2. Of those that a mesh axis runs over, the one named last changes fastest.
Arguments:
- residual_block: float32 [8, 512, 64, 256], P(None, 'gx', 'gy'), may hold values from -70 to 70
- diagonal: float32 [512, 64, 256], P('gx', 'gy'), may hold values from 0.5 to 4
Outputs:
- correction: float32 [8, 512, 64, 256], P(None, 'gx', 'gy')
- new_residual: float32 [8, 512, 64, 256], P(None, 'gx', 'gy')
- estimate: float32 [8], replicated
All inputs are finite; a program needn't handle non-finite values.
Results may differ from a plain program's by a relative error of at most 0.008.
Values sent between devices are 32-bit elements; how exact they have to be, the bound alone decides.
A program may use at most 32 MiB of HBM per device.

v0:
```python
import jax
import jax.numpy as jnp
import numpy as np
from jax import lax
from jax.sharding import Mesh
from jax.sharding import PartitionSpec as P

NRHS = 8
GX = ("gx_0", "gx_1")


WEIGHT_X = 0.4
WEIGHT_Y = 0.2
WEIGHT_Z = 0.1
CENTRE = 2.2
SCALE_POWER = 3.0
SHIFTS = (6.0, 1.5, 4.5, 3.0)
EPSILON = 1e-06


def padded_2(block, sides, width):
    for axis, dim in sides:
        count = lax.axis_size(axis)
        forward = [(i, i + 1) for i in range(count - 1)]
        backward = [(target, source) for source, target in forward]
        low = lax.ppermute(
            lax.slice_in_dim(block, block.shape[dim] - width, None, axis=dim), axis, forward
        )
        high = lax.ppermute(lax.slice_in_dim(block, 0, width, axis=dim), axis, backward)
        block = jnp.concatenate([low, block, high], axis=dim)
    return block


def sent_to_all(x, axis):
    count = lax.axis_size(axis)
    return lax.all_to_all(jnp.broadcast_to(x[None], (count, *x.shape)), axis, 0, 0, tiled=True)


def over_copies(x, axis):
    return sent_to_all(x, axis).sum(axis=0)


def one_axis_at_a_time(x, axes):
    for axis in axes:
        x = lax.psum(x, axis)
    return x


def apply_padded(padded, diag_inner, shift_now):
    along_z = jnp.pad(padded, ((0, 0), (0, 0), (0, 0), (1, 1)))
    sum_z = padded + WEIGHT_Z * (along_z[..., :-2] + along_z[..., 2:])
    sum_y = sum_z[:, :, 1:-1] + WEIGHT_Y * (sum_z[:, :, :-2] + sum_z[:, :, 2:])
    sum_x = sum_y[:, 1:-1] + WEIGHT_X * (sum_y[:, :-2] + sum_y[:, 2:])
    centre_cells = padded[:, 1:-1, 1:-1]
    return ((CENTRE + 1.0 + diag_inner - shift_now) * centre_cells - sum_x) / SCALE_POWER


def newton_table():
    blocks = len(SHIFTS)
    identity = np.eye(NRHS, dtype=np.float32)
    matrix = np.zeros(((blocks + 1) * NRHS, blocks * NRHS), np.float32)
    for block_index in range(blocks):
        low = block_index * NRHS
        matrix[low : low + NRHS, low : low + NRHS] = SHIFTS[block_index] * identity
        matrix[low + NRHS : low + 2 * NRHS, low : low + NRHS] = SCALE_POWER * identity
    return matrix


def solve_small(gram_full):
    highest = lax.Precision.HIGHEST
    newton = jnp.asarray(newton_table(), gram_full.dtype)
    image = jnp.dot(newton.T, jnp.dot(gram_full, newton, precision=highest), precision=highest)
    right_side = jnp.dot(newton.T, gram_full[:, :NRHS], precision=highest)
    scales = lax.rsqrt(jnp.diagonal(image) + EPSILON)
    scaled = image * scales[:, None] * scales[None, :]
    factor = jnp.linalg.cholesky(scaled)
    coeffs = scales[:, None] * jax.scipy.linalg.cho_solve(
        (factor, True), scales[:, None] * right_side
    )
    initial_sq = jnp.diagonal(gram_full)[:NRHS]
    estimate = (initial_sq - jnp.sum(right_side * coeffs, axis=0)) / initial_sq
    return (coeffs, jnp.dot(newton, coeffs, precision=highest), estimate)


def body(residual_block, diagonal):
    highest = lax.Precision.HIGHEST
    width_rhs, cells_x, cells_y, cells_z = residual_block.shape
    total_x = cells_x * lax.axis_size(GX)
    total_y = cells_y * lax.axis_size("gy")
    powers = [residual_block]
    depth = len(SHIFTS)
    outgoing = jnp.concatenate([residual_block, diagonal[None]], 0)
    extended = padded_2(outgoing, ((GX, 1), ("gy", 2)), depth)
    field_now = extended[:width_rhs]
    diag_wide = extended[width_rhs]
    coord_x = (
        lax.axis_index(GX) * cells_x - depth + jnp.arange(cells_x + 2 * depth, dtype=jnp.int32)
    )
    coord_y = (
        lax.axis_index("gy") * cells_y - depth + jnp.arange(cells_y + 2 * depth, dtype=jnp.int32)
    )
    inside_x = (coord_x >= 0) & (coord_x < total_x)
    inside_y = (coord_y >= 0) & (coord_y < total_y)
    for step_index, shift_now in enumerate(SHIFTS):
        margin = depth - 1 - step_index
        lower = depth - margin
        span_x = cells_x + 2 * margin
        span_y = cells_y + 2 * margin
        diag_now = diag_wide[lower : lower + span_x, lower : lower + span_y]
        field_now = apply_padded(field_now, diag_now, shift_now)
        inside = (
            inside_x[lower : lower + span_x][:, None] & inside_y[lower : lower + span_y][None, :]
        )
        field_now = jnp.where(inside[None, :, :, None], field_now, 0.0)
        powers.append(field_now[:, margin : margin + cells_x, margin : margin + cells_y])
    basis = jnp.concatenate(powers, 0).reshape(len(powers) * width_rhs, -1)
    local_gram = lax.dot_general(
        basis,
        basis,
        (((1,), (1,)), ((), ())),
        precision=highest,
        preferred_element_type=jnp.float32,
    )
    gram_part = over_copies(local_gram, "gy")
    gram_full = one_axis_at_a_time(gram_part, GX)
    coeffs, combined, estimate = solve_small(gram_full)
    kept = len(SHIFTS) * width_rhs
    correction = lax.dot_general(
        coeffs,
        basis[:kept],
        (((0,), (0,)), ((), ())),
        precision=highest,
        preferred_element_type=jnp.float32,
    )
    removed = lax.dot_general(
        combined,
        basis,
        (((0,), (0,)), ((), ())),
        precision=highest,
        preferred_element_type=jnp.float32,
    )
    new_residual = residual_block - removed.reshape(residual_block.shape)
    return (correction.reshape(residual_block.shape), new_residual, estimate)


def solution(mesh):
    split = Mesh(mesh.devices.reshape(32, 4, mesh.shape["gy"]), ("gx_0", "gx_1", "gy"))
    placed = (P(None, GX, "gy", None), P(GX, "gy", None))
    return jax.shard_map(
        body,
        mesh=split,
        in_specs=placed,
        out_specs=(P(None, GX, "gy", None), P(None, GX, "gy", None), P()),
        check_vma=False,
    )
```

profile of v0, /device:TPU:2, one launch (start us, length us, event | category | flops | bytes accessed | tf_op | source)
XLA Modules:
  0.0 205.0 jit_solution(18228487890761249168)
XLA Ops:
  0.6 1.1 constant_dynamic-update-slice_fusion.4
  1.8 0.8 broadcast_in_dim.61
  2.5 0.1 dynamic-update-slice.9
  2.7 1.3 collective-permute-start.1
  4.0 4.6 %collective-permute-start = (f32[9,4,8,256]{3,0,2,1:T(8,128)S(1)}, f32[9,4,8,256]{3,0,2,1:T(8,128)S(1)}, u32[]{:S(2)}, u32[]{:S(2)}) collective-permute-start(f32[9,4,8,256]{3,0,2,1:T(8,128)S(1)} %dynamic-update-slice.9), channel_id=1, source_target_pairs={{0,8},{8,16},{16,24},{24,32},{32,40},{40,48},{48,56},{56,64},{64,7... | collective-permute-start | bytes 884744 | tf_op jit(solution)/shard_map/ppermute | solution.py:26
  8.6 0.1 slice.194
  8.7 0.1 slice.211
  8.8 0.1 slice.193
  8.8 0.1 slice.210
  8.9 0.1 slice.224
  9.4 8.9 %collective-permute-done.1 = f32[9,4,8,256]{3,0,2,1:T(8,128)S(1)} collective-permute-done((f32[9,4,8,256]{3,0,2,1:T(8,128)S(1)}, f32[9,4,8,256]{3,0,2,1:T(8,128)S(1)}, u32[]{:S(2)}, u32[]{:S(2)}) %collective-permute-start.1) | collective-permute-done | bytes 294944 | tf_op jit(solution)/shard_map/ppermute | solution.py:29
  18.3 1.2 collective-permute-done
  19.4 0.1 pad_maximum_fusion.4
  19.6 0.1 fusion.57
  19.7 0.3 copy.41
  20.0 1.9 collective-permute-start.3
  21.9 0.3 copy.40
  22.2 2.4 %collective-permute-start.2 = (f32[9,12,4,256]{3,2,1,0:T(4,128)S(1)}, f32[9,12,4,256]{3,2,1,0:T(4,128)S(1)}, u32[]{:S(2)}, u32[]{:S(2)}) collective-permute-start(f32[9,12,4,256]{3,2,1,0:T(4,128)S(1)} %copy.40), channel_id=1, source_target_pairs={{0,1},{1,2},{2,3},{3,4},{4,5},{5,6},{6,7},{8,9},{9,10},{10,11},{11... | collective-permute-start | bytes 1327112 | tf_op jit(solution)/shard_map/ppermute | solution.py:26
  24.8 2.9 %collective-permute-done.3 = f32[9,12,4,256]{3,2,1,0:T(4,128)S(1)} collective-permute-done((f32[9,12,4,256]{3,2,1,0:T(4,128)S(1)}, f32[9,12,4,256]{3,2,1,0:T(4,128)S(1)}, u32[]{:S(2)}, u32[]{:S(2)}) %collective-permute-start.3) | collective-permute-done | bytes 442400 | tf_op jit(solution)/shard_map/ppermute | solution.py:29
  27.7 0.3 copy.43
  28.0 11.2 %collective-permute-done.2 = f32[9,12,4,256]{3,2,1,0:T(4,128)S(1)} collective-permute-done((f32[9,12,4,256]{3,2,1,0:T(4,128)S(1)}, f32[9,12,4,256]{3,2,1,0:T(4,128)S(1)}, u32[]{:S(2)}, u32[]{:S(2)}) %collective-permute-start.2) | collective-permute-done | bytes 442400 | tf_op jit(solution)/shard_map/ppermute | solution.py:26
  39.2 0.3 copy.42
  39.4 0.2 pad_maximum_fusion.6
  39.8 0.2 pad_maximum_fusion
  40.0 0.9 fusion.2
  40.8 0.2 fusion.4
  41.0 0.8 fusion.17
  41.8 0.7 fusion.12
  42.5 0.1 fusion.21
  42.6 0.3 fusion.29
  42.9 0.5 fusion.24
  43.5 0.2 fusion.39
  43.6 0.3 fusion.34
  44.0 0.1 fusion.47
  44.2 1.2 convolution_bitcast_fusion
  45.3 0.8 reshape.172
  46.1 3.3 %all-to-all-start = ((f32[8,1,1600]{2,1,0:T(1,128)}), f32[8,1,1600]{2,1,0:T(1,128)S(1)}, u32[]{:S(2)}, u32[]{:S(2)}) async-start(f32[8,1,1600]{2,1,0:T(1,128)} %reshape.172), calls=%async_computation | async-start | bytes 106496 | tf_op jit(solution)/shard_map/all_to_all | solution.py:36
  49.4 0.1 pad_maximum_fusion.5
  49.5 1.6 copy.59
  51.1 0.4 copy.61
  51.6 2.0 all-to-all-done
  53.5 0.5 broadcast.256
  54.0 0.8 reduce.6
  54.8 0.1 reshape.173
  55.0 121.0 %psum.14 = f32[40,40]{1,0:T(8,128)S(1)} all-reduce(f32[40,40]{1,0:T(8,128)S(1)} %reduce_sum.18), channel_id=1, replica_groups=mesh['gx_0'=32,'gx_1'=4,'gy'=8] {'gx_0'}, use_global_device_ids=true, to_apply=%region_1.2 | all-reduce | flops 1600 | bytes 12800 | tf_op jit(solution)/shard_map/psum | solution.py:45
  175.9 14.6 %psum.15 = f32[40,40]{1,0:T(8,128)S(1)} all-reduce(f32[40,40]{1,0:T(8,128)S(1)} %psum.14), channel_id=1, replica_groups=mesh['gx_0'=32,'gx_1'=4,'gy'=8] {'gx_1'}, use_global_device_ids=true, to_apply=%region_2.3 | all-reduce | flops 1600 | bytes 12800 | tf_op jit(solution)/shard_map/psum | solution.py:45
  190.5 0.2 fusion.48
  190.7 0.2 fusion.58
  191.0 0.1 fusion.59
  191.2 0.7 gather_fusion
  191.9 0.1 add_multiply_fusion
  192.0 2.9 %cholesky.16 = f32[32,32]{1,0:T(8,128)S(1)} custom-call(f32[32,32]{1,0:T(8,128)S(1)} %add_multiply_fusion), custom_call_target="Cholesky" | custom-call | tf_op jit(solution)/shard_map/jit(cholesky)/cholesky | solution.py:76
  194.9 0.6 compare_reduce_fusion
  195.6 0.7 fusion.50
  196.2 2.4 %custom-call.10 = f32[1,32,32]{1,2,0:T(8,128)S(1)} custom-call(f32[1,32,32]{2,1,0:T(8,128)S(1)} %fusion.50), custom_call_target="InvertDiagBlocksLowerTriangular" | custom-call | tf_op jit(solution)/shard_map/jit(_cho_solve)/triangular_solve | solution.py:77
  198.7 0.2 fusion.52
  198.8 0.3 multiply_reduce_fusion
  199.1 0.1 convolution_bitcast_fusion.1
  199.2 1.2 fusion.18
  200.4 0.8 copy.52
  201.2 1.5 fusion.7
  202.7 0.8 copy.53
  203.5 1.0 gather_fusion.1
  204.5 0.5 subtract_divide_fusion
  (32 shorter events, 1.0 us)
Async XLA Ops:
  2.7 15.6 %collective-permute-start.1 = (f32[9,4,8,256]{3,0,2,1:T(8,128)S(1)}, f32[9,4,8,256]{3,0,2,1:T(8,128)S(1)}, u32[]{:S(2)}, u32[]{:S(2)}) collective-permute-start(f32[9,4,8,256]{3,0,2,1:T(8,128)S(1)} %dynamic-update-slice.9), channel_id=1, source_target_pairs={{8,0},{16,8},{24,16},{32,24},{40,32},{48,40},{56,48},{64,56},{72,6... | collective-permute-start | bytes 884744 | tf_op jit(solution)/shard_map/ppermute | solution.py:29
  4.0 15.4 %collective-permute-start = (f32[9,4,8,256]{3,0,2,1:T(8,128)S(1)}, f32[9,4,8,256]{3,0,2,1:T(8,128)S(1)}, u32[]{:S(2)}, u32[]{:S(2)}) collective-permute-start(f32[9,4,8,256]{3,0,2,1:T(8,128)S(1)} %dynamic-update-slice.9), channel_id=1, source_target_pairs={{0,8},{8,16},{16,24},{24,32},{32,40},{40,48},{48,56},{56,64},{64,7... | collective-permute-start | bytes 884744 | tf_op jit(solution)/shard_map/ppermute | solution.py:26
  20.0 7.7 %collective-permute-start.3 = (f32[9,12,4,256]{3,2,1,0:T(4,128)S(1)}, f32[9,12,4,256]{3,2,1,0:T(4,128)S(1)}, u32[]{:S(2)}, u32[]{:S(2)}) collective-permute-start(f32[9,12,4,256]{3,2,1,0:T(4,128)S(1)} %copy.41), channel_id=1, source_target_pairs={{1,0},{2,1},{3,2},{4,3},{5,4},{6,5},{7,6},{9,8},{10,9},{11,10},{12... | collective-permute-start | bytes 1327112 | tf_op jit(solution)/shard_map/ppermute | solution.py:29
  22.2 16.9 %collective-permute-start.2 = (f32[9,12,4,256]{3,2,1,0:T(4,128)S(1)}, f32[9,12,4,256]{3,2,1,0:T(4,128)S(1)}, u32[]{:S(2)}, u32[]{:S(2)}) collective-permute-start(f32[9,12,4,256]{3,2,1,0:T(4,128)S(1)} %copy.40), channel_id=1, source_target_pairs={{0,1},{1,2},{2,3},{3,4},{4,5},{5,6},{6,7},{8,9},{9,10},{10,11},{11... | collective-permute-start | bytes 1327112 | tf_op jit(solution)/shard_map/ppermute | solution.py:26
  46.1 7.4 %all-to-all-start = ((f32[8,1,1600]{2,1,0:T(1,128)}), f32[8,1,1600]{2,1,0:T(1,128)S(1)}, u32[]{:S(2)}, u32[]{:S(2)}) async-start(f32[8,1,1600]{2,1,0:T(1,128)} %reshape.172), calls=%async_computation | async-start | bytes 106496 | tf_op jit(solution)/shard_map/all_to_all | solution.py:36
  51.1 139.4 %copy-start.2 = (f32[40,32]{1,0:T(8,128)S(1)}, f32[40,32]{1,0:T(8,128)}, u32[]{:S(2)}) copy-start(f32[40,32]{1,0:T(8,128)} %constant.137.clone) | copy-start | bytes 15364
  51.6 147.7 %copy-start = (f32[4,8,32,256]{3,2,1,0:T(8,128)S(1)}, f32[4,8,32,256]{3,2,1,0:T(8,128)}, u32[]{:S(2)}) copy-start(f32[4,8,32,256]{3,2,1,0:T(8,128)} %copy.59) | copy-start | bytes 3145732
  191.1 10.1 %copy-start.1 = (f32[8,4,8,256]{3,2,1,0:T(8,128)S(1)}, f32[8,4,8,256]{3,2,1,0:T(8,128)}, u32[]{:S(2)}) copy-start(f32[8,4,8,256]{3,2,1,0:T(8,128)} %param.3) | copy-start | bytes 786436
where the time goes:
time: 205 us
  blocking collectives  136 us (66%)
  waiting for transfers between devices  26.1 us (13%)
  starting transfers between devices  13.5 us (7%)
  other arithmetic  13.1 us (6%)
  local copies, waits for them, and re-layouts  10.8 us (5%)
  matrix products  4.96 us (2%)
    psum x2, blocking collectives, one_axis_at_a_time(): x = lax.psum(x, axis)  136 us
    ppermute x2, waiting for transfers between devices, padded_2(): lax.ppermute(lax.slice_in_dim(block, block.shape[dim] - width, None, axis...  12.3 us
    ppermute x2, waiting for transfers between devices, padded_2(): lax.ppermute(lax.slice_in_dim(block, 0, width, axis=dim), axis, backward)  11.8 us
    ppermute x2, starting transfers between devices, padded_2(): lax.ppermute(lax.slice_in_dim(block, block.shape[dim] - width, None, axis...  6.99 us
    unnamed x17, local copies, waits for them, and re-layouts  5.73 us
  transfers between devices with their start and end apart: 5, of which 5 were waited for; matrix products, arithmetic and copies ran while one was open for 2% of the time, Pallas kernels for 0%

commit v1 on v0

--- a/solution.py
+++ b/solution.py
@@ -1,12 +1,15 @@
+import functools
+
 import jax
 import jax.numpy as jnp
 import numpy as np
 from jax import lax
-from jax.sharding import Mesh
+from jax.experimental import pallas as pl
+from jax.experimental.pallas import tpu as pltpu
 from jax.sharding import PartitionSpec as P
 
 NRHS = 8
-GX = ("gx_0", "gx_1")
+GX = "gx"
 
 
 WEIGHT_X = 0.4
@@ -31,19 +34,90 @@
     return block
 
 
-def sent_to_all(x, axis):
-    count = lax.axis_size(axis)
-    return lax.all_to_all(jnp.broadcast_to(x[None], (count, *x.shape)), axis, 0, 0, tiled=True)
-
-
-def over_copies(x, axis):
-    return sent_to_all(x, axis).sum(axis=0)
-
-
-def one_axis_at_a_time(x, axes):
-    for axis in axes:
-        x = lax.psum(x, axis)
-    return x
+def moments_of(gram):
+    n = NRHS
+    last = len(SHIFTS)
+    rows = [gram[:n, j * n : (j + 1) * n] for j in range(last + 1)]
+    rows += [gram[last * n :, j * n : (j + 1) * n] for j in range(1, last + 1)]
+    flat = jnp.stack(rows).reshape(-1)
+    return jnp.pad(flat, (0, ROWS * 128 - flat.shape[0])).reshape(ROWS, 128)
+
+
+def from_moments(words):
+    n, last = NRHS, len(SHIFTS)
+    blocks = words.reshape(-1)[: (2 * last + 1) * n * n].reshape(2 * last + 1, n, n)
+    table = {(0, j): blocks[j] for j in range(last + 1)}
+    table |= {(last, j): blocks[last + j] for j in range(1, last + 1)}
+    table[last, 0] = blocks[last].T
+    for i in range(1, last):
+        table[i, last] = blocks[last + i].T
+    for i in range(last - 1):
+        for j in range(last):
+            factor = (SHIFTS[j] - SHIFTS[i]) / SCALE_POWER
+            table[i + 1, j] = table[i, j + 1] + factor * table[i, j]
+    return jnp.block([[table[i, j] for j in range(last + 1)] for i in range(last + 1)])
+
+
+MESH = pl.DeviceIdType.MESH
+ROWS = 5
+
+
+def sum_everywhere(sides, x_ref, out_ref, plane, line, plane_sum, send_sem, plane_sem, line_sem):
+    nz, ny, nx = sides
+    gx, gy = lax.axis_index("gx"), lax.axis_index("gy")
+    z, y, x, core = gx // ny, gx % ny, gy // 2, gy % 2
+
+    def device(dz, dy, dx, dc):
+        return ((z + dz) % nz * ny + (y + dy) % ny, (x + dx) % nx * 2 + (core + dc) % 2)
+
+    planes = [(0, dy, dx, dc) for dy in range(ny) for dx in range(nx) for dc in range(2)][1:]
+    lines = sorted([(dz, 0, 0, 0) for dz in range(1, nz)], key=lambda m: -min(m[0], nz - m[0]))
+    barrier = pltpu.get_barrier_semaphore()
+    for move in planes + lines:
+        pl.semaphore_signal(barrier, inc=1, device_id=device(*move), device_id_type=MESH)
+    pl.semaphore_wait(barrier, len(planes) + len(lines))
+
+    def exchange(src, slots, moves, sem):
+        def copy(k, move):
+            return pltpu.make_async_remote_copy(
+                src_ref=src.at[pl.ds(0, ROWS)],
+                dst_ref=slots.at[k],
+                send_sem=send_sem,
+                recv_sem=sem,
+                device_id=device(*move),
+                device_id_type=MESH,
+            )
+
+        for k, move in enumerate(moves):
+            copy(k, move).start()
+        for end in (send_sem, sem):
+            pltpu.make_async_copy(slots, slots, end).wait()
+
+    exchange(x_ref, plane, planes, plane_sem)
+    plane_sum[...] = x_ref[...] + jnp.sum(plane[...], axis=0)
+    exchange(plane_sum, line, lines, line_sem)
+    out_ref[...] = plane_sum[...] + jnp.sum(line[...], axis=0)
+
+
+def all_reduce(words):
+    ny = lax.axis_size("gx") // 32
+    sides = (32, ny, lax.axis_size("gy") // 2)
+    vmem = pl.BlockSpec(memory_space=pltpu.VMEM)
+    return pl.pallas_call(
+        functools.partial(sum_everywhere, sides),
+        out_shape=jax.ShapeDtypeStruct((ROWS, 128), jnp.float32),
+        in_specs=[vmem],
+        out_specs=vmem,
+        scratch_shapes=[
+            pltpu.VMEM((sides[1] * sides[2] * 2 - 1, ROWS, 128), jnp.float32),
+            pltpu.VMEM((sides[0] - 1, ROWS, 128), jnp.float32),
+            pltpu.VMEM((ROWS, 128), jnp.float32),
+            pltpu.SemaphoreType.DMA,
+            pltpu.SemaphoreType.DMA,
+            pltpu.SemaphoreType.DMA,
+        ],
+        compiler_params=pltpu.CompilerParams(collective_id=0, has_side_effects=True),
+    )(words)
 
 
 def apply_padded(padded, diag_inner, shift_now):
@@ -121,8 +195,7 @@
         precision=highest,
         preferred_element_type=jnp.float32,
     )
-    gram_part = over_copies(local_gram, "gy")
-    gram_full = one_axis_at_a_time(gram_part, GX)
+    gram_full = from_moments(all_reduce(moments_of(local_gram)))
     coeffs, combined, estimate = solve_small(gram_full)
     kept = len(SHIFTS) * width_rhs
     correction = lax.dot_general(
@@ -144,11 +217,10 @@
 
 
 def solution(mesh):
-    split = Mesh(mesh.devices.reshape(32, 4, mesh.shape["gy"]), ("gx_0", "gx_1", "gy"))
     placed = (P(None, GX, "gy", None), P(GX, "gy", None))
     return jax.shard_map(
         body,
-        mesh=split,
+        mesh=mesh,
         in_specs=placed,
         out_specs=(P(None, GX, "gy", None), P(None, GX, "gy", None), P()),
         check_vma=False,

time: 205 us -> 112 us (0.55)
  the two profiles are of different devices: /device:TPU:2 before, /device:TPU:1 now
where the time goes in v1:
time: 112 us; the launch traced here: 111 us
  Pallas kernels  45 us (40%)
  starting transfers between devices  24.4 us (22%)
  local copies, waits for them, and re-layouts  12.7 us (11%)
  other arithmetic  12.5 us (11%)
  waiting for transfers between devices  10.1 us (9%)
  matrix products  4.97 us (4%)
    pallas_call x1, Pallas kernels, all_reduce(): pl.pallas_call(functools.partial(sum_everywhere, sides), out_shape=jax.Sh...  45 us
    ppermute x2, starting transfers between devices, padded_2(): lax.ppermute(lax.slice_in_dim(block, 0, width, axis=dim), axis, backward)  17.8 us
    ppermute x2, starting transfers between devices, padded_2(): lax.ppermute(lax.slice_in_dim(block, block.shape[dim] - width, None, axis...  6.6 us
    ppermute x2, waiting for transfers between devices, padded_2(): lax.ppermute(lax.slice_in_dim(block, block.shape[dim] - width, None, axis...  6.27 us
    unnamed x30, local copies, waits for them, and re-layouts  5.24 us
    ppermute x2, waiting for transfers between devices, padded_2(): lax.ppermute(lax.slice_in_dim(block, 0, width, axis=dim), axis, backward)  3.8 us
    another operation x3, other arithmetic, solve_small(): factor = jnp.linalg.cholesky(scaled)  3.6 us
    another operation x2, other arithmetic, solve_small(): jax.scipy.linalg.cho_solve((factor, True), scales[:, None] * right_side)  3.09 us
  transfers between devices with their start and end apart: 4, of which 3 were waited for; matrix products, arithmetic and copies ran while one was open for 1% of the time, Pallas kernels for 0%

profile of v1, /device:TPU:1, one launch (start us, length us, event | category | flops | bytes accessed | tf_op | source)
XLA Modules:
  0.0 110.7 jit_solution(13885376980804637814)
XLA Ops:
  0.6 1.1 %constant_dynamic-update-slice_fusion.4 = (f32[40,4,8,256]{3,0,2,1:T(8,128)S(1)}, f32[9,4,8,256]{3,0,2,1:T(8,128)S(1)}, f32[8,4,8,256]{3,0,2,1:T(8,128)S(1)}) fusion(f32[8,4,8,256]{3,2,1,0:T(8,128)} %param.3), kind=kLoop, calls=%fused_computation.85 | loop fusion | bytes 1048576
  1.8 0.8 broadcast_in_dim.59
  2.5 0.1 dynamic-update-slice.23
  2.7 1.3 %collective-permute-start.1 = (f32[9,4,8,256]{3,0,2,1:T(8,128)S(1)}, f32[9,4,8,256]{3,0,2,1:T(8,128)S(1)}, u32[]{:S(2)}, u32[]{:S(2)}) collective-permute-start(f32[9,4,8,256]{3,0,2,1:T(8,128)S(1)} %dynamic-update-slice.23), channel_id=1, source_target_pairs={{8,0},{16,8},{24,16},{32,24},{40,32},{48,40},{56,48},{64,56},{72,6... | collective-permute-start | bytes 884744 | tf_op jit(solution)/shard_map/ppermute | solution.py:32
  4.0 4.7 %collective-permute-start = (f32[9,4,8,256]{3,0,2,1:T(8,128)S(1)}, f32[9,4,8,256]{3,0,2,1:T(8,128)S(1)}, u32[]{:S(2)}, u32[]{:S(2)}) collective-permute-start(f32[9,4,8,256]{3,0,2,1:T(8,128)S(1)} %dynamic-update-slice.23), channel_id=1, source_target_pairs={{0,8},{8,16},{16,24},{24,32},{32,40},{40,48},{48,56},{56,64},{64,7... | collective-permute-start | bytes 884744 | tf_op jit(solution)/shard_map/ppermute | solution.py:29
  8.7 0.1 slice.283
  8.8 0.1 slice.300
  8.9 0.1 slice.282
  9.5 3.8 %collective-permute-done.1 = f32[9,4,8,256]{3,0,2,1:T(8,128)S(1)} collective-permute-done((f32[9,4,8,256]{3,0,2,1:T(8,128)S(1)}, f32[9,4,8,256]{3,0,2,1:T(8,128)S(1)}, u32[]{:S(2)}, u32[]{:S(2)}) %collective-permute-start.1) | collective-permute-done | bytes 294944 | tf_op jit(solution)/shard_map/ppermute | solution.py:32
  13.3 1.5 %collective-permute-done = f32[9,4,8,256]{3,0,2,1:T(8,128)S(1)} collective-permute-done((f32[9,4,8,256]{3,0,2,1:T(8,128)S(1)}, f32[9,4,8,256]{3,0,2,1:T(8,128)S(1)}, u32[]{:S(2)}, u32[]{:S(2)}) %collective-permute-start) | collective-permute-done | bytes 294944 | tf_op jit(solution)/shard_map/ppermute | solution.py:29
  14.8 0.1 pad_maximum_fusion.4
  14.9 0.1 fusion.57
  15.0 0.3 copy.42
  15.3 16.5 %collective-permute-start.3 = (f32[9,12,4,256]{3,2,1,0:T(4,128)S(1)}, f32[9,12,4,256]{3,2,1,0:T(4,128)S(1)}, u32[]{:S(2)}, u32[]{:S(2)}) collective-permute-start(f32[9,12,4,256]{3,2,1,0:T(4,128)S(1)} %copy.42), channel_id=1, source_target_pairs={{1,0},{2,1},{3,2},{4,3},{5,4},{6,5},{7,6},{9,8},{10,9},{11,10},{12... | collective-permute-start | bytes 1327112 | tf_op jit(solution)/shard_map/ppermute | solution.py:32
  31.8 0.3 copy.41
  32.1 1.9 %collective-permute-start.2 = (f32[9,12,4,256]{3,2,1,0:T(4,128)S(1)}, f32[9,12,4,256]{3,2,1,0:T(4,128)S(1)}, u32[]{:S(2)}, u32[]{:S(2)}) collective-permute-start(f32[9,12,4,256]{3,2,1,0:T(4,128)S(1)} %copy.41), channel_id=1, source_target_pairs={{0,1},{1,2},{2,3},{3,4},{4,5},{5,6},{6,7},{8,9},{9,10},{10,11},{11... | collective-permute-start | bytes 1327112 | tf_op jit(solution)/shard_map/ppermute | solution.py:29
  34.2 0.3 copy.44
  34.5 4.8 %collective-permute-done.2 = f32[9,12,4,256]{3,2,1,0:T(4,128)S(1)} collective-permute-done((f32[9,12,4,256]{3,2,1,0:T(4,128)S(1)}, f32[9,12,4,256]{3,2,1,0:T(4,128)S(1)}, u32[]{:S(2)}, u32[]{:S(2)}) %collective-permute-start.2) | collective-permute-done | bytes 442400 | tf_op jit(solution)/shard_map/ppermute | solution.py:29
  39.3 0.3 copy.43
  39.6 0.2 pad_maximum_fusion.6
  39.9 0.2 pad_maximum_fusion
  40.1 0.9 fusion.2
  40.9 0.2 fusion.4
  41.1 1.0 fusion.17
  42.1 0.7 fusion.12
  42.8 0.1 fusion.21
  42.9 0.3 fusion.29
  43.1 0.5 fusion.24
  43.7 0.1 fusion.39
  43.9 0.3 fusion.34
  44.3 0.1 fusion.47
  44.4 1.2 %convolution_bitcast_fusion = f32[40,40]{1,0:T(8,128)S(1)} fusion(f32[40,4,8,256]{3,0,2,1:T(8,128)S(1)} %get-tuple-element.30), kind=kOutput, calls=%fused_computation.32 | convolution fusion | flops 157286400 | bytes 1317120 | tf_op jit(solution)/shard_map/dot_general | solution.py:191
  46.2 0.1 reshape.200
  46.3 0.6 pad_bitcast_fusion.x_ref
  46.9 45.0 %shard_map.58 = f32[5,128]{1,0:T(8,128)} custom-call(f32[5,128]{1,0:T(8,128)} %pad_bitcast_fusion.x_ref), custom_call_target="tpu_custom_call" | custom-call | tf_op jit(solution)/shard_map/pallas_call | solution.py:106
  91.9 0.8 slice.345
  93.0 0.1 concatenate.51
  94.2 0.1 concatenate.52
  94.3 0.1 concatenate.53
  94.4 0.1 concatenate.54
  94.5 0.1 concatenate.55
  94.6 0.2 fusion.48
  94.8 0.2 fusion.59
  95.0 0.1 pad_maximum_fusion.5
  95.1 0.6 copy.90
  95.7 0.1 fusion.60
  95.8 0.1 copy.71
  95.9 0.7 gather_fusion
  96.7 0.1 add_multiply_fusion
  96.7 2.9 %cholesky.16 = f32[32,32]{1,0:T(8,128)S(1)} custom-call(f32[32,32]{1,0:T(8,128)S(1)} %add_multiply_fusion), custom_call_target="Cholesky" | custom-call | tf_op jit(solution)/shard_map/jit(cholesky)/cholesky | solution.py:150
  99.7 0.6 compare_reduce_fusion
  100.3 0.7 fusion.50
  101.0 2.4 %custom-call.10 = f32[1,32,32]{1,2,0:T(8,128)S(1)} custom-call(f32[1,32,32]{2,1,0:T(8,128)S(1)} %fusion.50), custom_call_target="InvertDiagBlocksLowerTriangular" | custom-call | tf_op jit(solution)/shard_map/jit(_cho_solve)/triangular_solve | solution.py:151
  103.4 0.2 fusion.52
  103.6 0.3 multiply_reduce_fusion
  103.9 0.1 convolution_bitcast_fusion.1
  104.0 1.2 %fusion.18 = f32[8,4,8,256]{3,0,2,1:T(8,128)S(1)} fusion(f32[4,8,256,32]{2,1,0,3:T(8,128)S(1)} %bitcast.115, f32[32,8]{0,1:T(8,128)S(1)} %get-tuple-element.48), kind=kOutput, calls=%fused_computation.36 | convolution fusion | flops 25165824 | bytes 1311744 | tf_op jit(solution)/shard_map/dot_general | solution.py:201
  105.2 0.8 copy.78
  106.0 0.4 copy.92
  106.4 0.5 copy-done
  106.9 1.5 %fusion.7 = f32[8,4,8,256]{3,0,2,1:T(8,128)S(1)} fusion(f32[8,40,1,1]{1,0,3,2:T(8,128)S(1)} %convolution_bitcast_fusion.1, f32[4,8,256,40]{2,1,0,3:T(8,128)S(1)} %bitcast.114, f32[8,4,8,256]{3,2,1,0:T(8,128)S(1)} %copy-done), kind=kOutput, calls=%fused_computation.21 | convolution fusion | flops 31522816 | bytes 1836288 | tf_op jit(solution)/shard_map/dot_general | solution.py:208
  108.4 0.8 copy.79
  109.2 1.0 gather_fusion.1
  110.2 0.5 subtract_divide_fusion
  (68 shorter events, 3.1 us)
Async XLA Ops:
  2.7 10.6 %collective-permute-start.1 = (f32[9,4,8,256]{3,0,2,1:T(8,128)S(1)}, f32[9,4,8,256]{3,0,2,1:T(8,128)S(1)}, u32[]{:S(2)}, u32[]{:S(2)}) collective-permute-start(f32[9,4,8,256]{3,0,2,1:T(8,128)S(1)} %dynamic-update-slice.23), channel_id=1, source_target_pairs={{8,0},{16,8},{24,16},{32,24},{40,32},{48,40},{56,48},{64,56},{72,6... | collective-permute-start | bytes 884744 | tf_op jit(solution)/shard_map/ppermute | solution.py:32
  4.0 10.8 %collective-permute-start = (f32[9,4,8,256]{3,0,2,1:T(8,128)S(1)}, f32[9,4,8,256]{3,0,2,1:T(8,128)S(1)}, u32[]{:S(2)}, u32[]{:S(2)}) collective-permute-start(f32[9,4,8,256]{3,0,2,1:T(8,128)S(1)} %dynamic-update-slice.23), channel_id=1, source_target_pairs={{0,8},{8,16},{16,24},{24,32},{32,40},{40,48},{48,56},{56,64},{64,7... | collective-permute-start | bytes 884744 | tf_op jit(solution)/shard_map/ppermute | solution.py:29
  15.3 18.9 %collective-permute-start.3 = (f32[9,12,4,256]{3,2,1,0:T(4,128)S(1)}, f32[9,12,4,256]{3,2,1,0:T(4,128)S(1)}, u32[]{:S(2)}, u32[]{:S(2)}) collective-permute-start(f32[9,12,4,256]{3,2,1,0:T(4,128)S(1)} %copy.42), channel_id=1, source_target_pairs={{1,0},{2,1},{3,2},{4,3},{5,4},{6,5},{7,6},{9,8},{10,9},{11,10},{12... | collective-permute-start | bytes 1327112 | tf_op jit(solution)/shard_map/ppermute | solution.py:32
  32.1 7.2 %collective-permute-start.2 = (f32[9,12,4,256]{3,2,1,0:T(4,128)S(1)}, f32[9,12,4,256]{3,2,1,0:T(4,128)S(1)}, u32[]{:S(2)}, u32[]{:S(2)}) collective-permute-start(f32[9,12,4,256]{3,2,1,0:T(4,128)S(1)} %copy.41), channel_id=1, source_target_pairs={{0,1},{1,2},{2,3},{3,4},{4,5},{5,6},{6,7},{8,9},{9,10},{10,11},{11... | collective-permute-start | bytes 1327112 | tf_op jit(solution)/shard_map/ppermute | solution.py:29
  44.4 50.2 %copy-start.1 = (f32[40,32]{1,0:T(8,128)S(1)}, f32[40,32]{1,0:T(8,128)}, u32[]{:S(2)}) copy-start(f32[40,32]{1,0:T(8,128)} %constant.143.clone) | copy-start | bytes 15364
  106.0 0.9 copy-start

commit v2 on v0

v2 whole, which is shorter than its diff:
```python
import functools

import jax
import jax.numpy as jnp
from jax import lax
from jax.experimental import pallas as pl
from jax.experimental.pallas import tpu as pltpu
from jax.sharding import PartitionSpec as P

NRHS = 8
WEIGHT_X = 0.4
WEIGHT_Y = 0.2
WEIGHT_Z = 0.1
CENTRE = 2.2
SCALE_POWER = 3.0
SHIFTS = (6.0, 1.5, 4.5, 3.0)
DEPTH = len(SHIFTS)
BLOCKS = DEPTH + 1
MOMENTS = 2 * DEPTH + 1
ROWS = 4
LANES = 128
TILE = (8, LANES)
SPAN = 3 * DEPTH
MESH = pl.DeviceIdType.MESH
PLANE_SIDES = (4, 4)
VMEM_BYTES = 16 << 20


def iotas():
    return lax.broadcasted_iota(jnp.int32, TILE, 0), lax.broadcasted_iota(jnp.int32, TILE, 1)


def tiles_of(ref, *index):
    return [ref[(*index, slice(None), slice(h, h + LANES))] for h in (0, LANES)]


def next_plane(before, here, after, centre, factors, own_only):
    row, lane = iotas()
    first, last = row == 0, row == 7
    summed = [b + WEIGHT_X * (a + c) for a, b, c in zip(before, here, after)]
    down = [pltpu.roll(t, 1, 0) for t in summed]
    up = [pltpu.roll(t, 7, 0) for t in summed]
    out = []
    for tile in range(0, 2 if own_only else 4, 2):
        other = 2 - tile
        halves = []
        for h in (0, 1):
            low = jnp.where(first, down[other + h], down[tile + h])
            high = jnp.where(last, up[other + h], up[tile + h])
            halves.append(summed[tile + h] + WEIGHT_Y * (low + high))
        right = [pltpu.roll(t, 1, 1) for t in halves]
        left = [pltpu.roll(t, LANES - 1, 1) for t in halves]
        start, end = lane == 0, lane == LANES - 1
        low = [jnp.where(start, 0.0, right[0]), jnp.where(start, right[0], right[1])]
        high = [jnp.where(end, left[1], left[0]), jnp.where(end, 0.0, left[1])]
        for h in (0, 1):
            total = halves[h] + WEIGHT_Z * (low[h] + high[h])
            out.append(centre[tile + h] * here[tile + h] - factors[tile // 2] * total)
    return out


def moments_kernel(
    sides, residual, diagonal, basis, total, own, edge, centres, message, plane, line, plane_sum,
    load_sem, x_sem, y_sem, sent_x, sent_y, plane_sem, line_sem, sent_plane, sent_line, round_sem,
):
    nz, ny, nx = sides
    gx, gy = lax.axis_index("gx"), lax.axis_index("gy")
    z, y, x, core = gx // ny, gx % ny, gy // 2, gy % 2
    count_x, count_y = nz * ny, nx * 2

    def device(dz=0, dy=0, dx=0, dc=0):
        return ((z + dz) % nz * ny + (y + dy) % ny, (x + dx) % nx * 2 + (core + dc) % 2)

    def other(dz=0, dy=0, dx=0, dc=0):
        return bool(dz % nz or dy % ny or dx % nx or dc % 2)

    sides_x = [((gx - 1) % count_x, gy), ((gx + 1) % count_x, gy)]
    sides_y = [(gx, (gy - 1) % count_y), (gx, (gy + 1) % count_y)]

    for slot in range(NRHS + 1):
        source = residual.at[slot - 1] if slot else diagonal
        pltpu.make_async_copy(source, own.at[slot, pl.ds(DEPTH, DEPTH)], load_sem.at[slot]).start()

    barrier = pltpu.get_barrier_semaphore()
    near = sides_x + sides_y
    near += [device(**{axis: step}) for axis in ("dz", "dy", "dx") for step in (1, -1)]
    for one in near:
        pl.semaphore_signal(barrier, inc=1, device_id=one, device_id_type=MESH)
    message[...] = jnp.zeros(TILE, jnp.float32)
    pl.semaphore_wait(barrier, len(near))

    rounds = [
        [dict(dx=1), dict(dx=-1), dict(dy=1), dict(dy=-1), dict(dz=1), dict(dz=-1)],
        [dict(dx=1), dict(dx=-1), dict(dx=2), dict(dz=2), dict(dz=-2)],
        [dict(dc=1), dict(dz=4), dict(dz=-4)],
        [dict(dz=8), dict(dz=-8)],
    ]
    rounds = [[move for move in moves if other(**move)] for moves in rounds]

    def tell(n):
        for move in rounds[n]:
            pl.semaphore_signal(round_sem.at[n], inc=1, device_id=device(**move), device_id_type=MESH)

    def hear(n):
        if rounds[n]:
            pl.semaphore_wait(round_sem.at[n], len(rounds[n]))

    tell(0)

    def send_y(slot, planes):
        for near_y, half in zip(sides_y, (0, 4)):
            pltpu.make_async_remote_copy(
                src_ref=own.at[slot, planes, pl.ds(half, 4)],
                dst_ref=edge.at[slot, planes, pl.ds(half, 4)],
                send_sem=sent_y,
                recv_sem=y_sem.at[slot],
                device_id=near_y,
                device_id_type=MESH,
            ).start()

    def send_own(slot, _):
        here = own.at[slot, pl.ds(DEPTH, DEPTH)]
        pltpu.make_async_copy(here, here, load_sem.at[slot]).wait()
        for near_x, start in zip(sides_x, (2 * DEPTH, 0)):
            pltpu.make_async_remote_copy(
                src_ref=here,
                dst_ref=own.at[slot, pl.ds(start, DEPTH)],
                send_sem=sent_x,
                recv_sem=x_sem.at[slot],
                device_id=near_x,
                device_id_type=MESH,
            ).start()
        send_y(slot, pl.ds(DEPTH, DEPTH))
        return 0

    lax.fori_loop(0, NRHS + 1, send_own, 0)

    def pass_on(slot):
        both = own.at[slot, pl.ds(0, 2 * DEPTH)]
        pltpu.make_async_copy(both, both, x_sem.at[slot]).wait()
        send_y(slot, pl.ds(0, DEPTH))
        send_y(slot, pl.ds(2 * DEPTH, DEPTH))

    def whole(slot):
        pltpu.make_async_copy(edge.at[slot], edge.at[slot], y_sem.at[slot]).wait()

    row, lane = iotas()

    def flag(test):
        return jnp.where(test, 1.0, 0.0).astype(jnp.float32)

    around = jnp.where(row < 4, flag(gy < count_y - 1), flag(gy > 0))
    outside = {-1: flag(gx > 0), 0: jnp.float32(1.0), 1: flag(gx < count_x - 1)}

    def masks(plane_x, scale):
        side = outside[plane_x // DEPTH - 1] * scale
        return jnp.full(TILE, side, jnp.float32), around * side

    def prepare():
        for plane_x in range(1, SPAN - 1):
            tiles = tiles_of(own, 0, plane_x) + tiles_of(edge, 0, plane_x)
            for step, shift in enumerate(SHIFTS):
                if step < plane_x < SPAN - 1 - step:
                    for q, t in enumerate(tiles):
                        centres[step, plane_x, q] = (t + (CENTRE + 1.0 - shift)) * (1.0 / SCALE_POWER)

    def extend(slot):
        field = slot - 1
        levels = [{} for _ in range(BLOCKS)]
        for plane_x in range(SPAN):
            tiles = tiles_of(own, slot, plane_x) + tiles_of(edge, slot, plane_x)
            inner, outer = masks(plane_x, 1.0)
            if DEPTH <= plane_x < 2 * DEPTH:
                for h in (0, 1):
                    basis[0, field, plane_x - DEPTH, :, h * LANES : (h + 1) * LANES] = tiles[h]
            else:
                tiles[:2] = [t * inner for t in tiles[:2]]
            levels[0][plane_x] = tiles[:2] + [t * outer for t in tiles[2:]]
            for step in range(DEPTH):
                middle = plane_x - 1 - step
                if not step < middle < SPAN - 1 - step:
                    continue
                own_only = step == DEPTH - 1
                tiles = next_plane(
                    *(levels[step][middle + d] for d in (-1, 0, 1)),
                    [centres[step, middle, q] for q in range(2 if own_only else 4)],
                    masks(middle, 1.0 / SCALE_POWER),
                    own_only,
                )
                levels[step + 1][middle] = tiles
                if DEPTH <= middle < 2 * DEPTH:
                    for h in (0, 1):
                        basis[step + 1, field, middle - DEPTH, :, h * LANES : (h + 1) * LANES] = tiles[h]

    spots = [(plane_x, h) for plane_x in range(DEPTH) for h in (0, 1)]

    def at(power, field, spot):
        plane_x, h = spot
        return basis[power, field, plane_x, :, h * LANES : (h + 1) * LANES]

    def measure(slot):
        field = slot - 1
        zero = jnp.zeros(TILE, jnp.float32)

        def pair(e, columns):
            sums = [None] * MOMENTS
            for spot in spots:
                first, last = at(0, field, spot), at(DEPTH, field, spot)
                for power in range(BLOCKS):
                    value = at(power, e, spot)
                    terms = [(power, first * value)]
                    if power:
                        terms.append((DEPTH + power, last * value))
                    for k, term in terms:
                        sums[k] = term if sums[k] is None else sums[k] + term
            out = []
            for k in range(MOMENTS):
                s = sums[k]
                for step in (4, 2, 1):
                    s = s + pltpu.roll(s, step, 0)
                out.append(jnp.where(row == e, s, columns[k]))
            return tuple(out)

        columns = lax.fori_loop(0, field + 1, pair, (zero,) * MOMENTS)
        placed = zero
        for k in range(MOMENTS):
            column = jnp.broadcast_to(jnp.sum(columns[k], axis=1, keepdims=True), TILE)
            low = pltpu.roll(column, 4, 0)
            place = 72 + 8 * k + field if k < 7 else 72 + 8 * (k - 7) + field - 4
            place = jnp.where(field >= 4, place, -1)
            placed = placed + jnp.where((lane == 8 * k + field) & (row < 4), column, 0.0)
            placed = placed + jnp.where((lane == place) & (row < 4), low, 0.0)
        message[...] = message[...] + placed

    pass_on(0)
    pass_on(1)
    hear(0)
    tell(1)
    whole(0)
    prepare()

    def advance(slot, _):
        @pl.when(slot <= NRHS)
        def _():
            pass_on(slot)

        @pl.when(slot == 4)
        def _():
            hear(1)
            tell(2)

        @pl.when(slot == 7)
        def _():
            hear(2)
            tell(3)

        @pl.when(slot >= LAG + 1)
        def _():
            whole(slot - LAG)
            extend(slot - LAG)
            measure(slot - LAG)

        return 0

    lax.fori_loop(2, NRHS + 1 + LAG, advance, 0)

    def exchange(src, slots, moves, sent, sem):
        for k, move in enumerate(moves):
            pltpu.make_async_remote_copy(
                src_ref=src.at[pl.ds(0, ROWS)],
                dst_ref=slots.at[k],
                send_sem=sent,
                recv_sem=sem,
                device_id=device(*move),
                device_id_type=MESH,
            ).start()
        pltpu.make_async_copy(slots, slots, sem).wait()

    planes = [(0, dy, dx, dc) for dy in range(ny) for dx in range(nx) for dc in range(2)][1:]
    lines = sorted([(dz, 0, 0, 0) for dz in range(1, nz)], key=lambda m: -min(m[0], nz - m[0]))
    exchange(message, plane, planes, sent_plane, plane_sem)
    plane_sum[...] = message[: ROWS] + jnp.sum(plane[...], axis=0)
    hear(3)
    exchange(plane_sum, line, lines, sent_line, line_sem)
    total[: ROWS] = plane_sum[...] + jnp.sum(line[...], axis=0)
    total[ROWS:] = jnp.zeros((8 - ROWS, LANES), jnp.float32)

    for buffer, sem in ((own.at[:, pl.ds(0, 2 * DEPTH)], sent_x), (edge, sent_y), (plane, sent_plane), (line, sent_line)):
        pltpu.make_async_copy(buffer, buffer, sem).wait()


LAG = 3


def add_into(table, factor, terms):
    for k, value in terms.items():
        table[k] = table.get(k, 0.0) + factor * value


def expansions():
    gram = {}
    for j in range(BLOCKS):
        gram[0, j] = {j: 1.0}
        gram[DEPTH, j] = gram[j, DEPTH] = {DEPTH + j: 1.0}
    for i in range(DEPTH - 1):
        for j in range(DEPTH):
            gram[i + 1, j] = {}
            add_into(gram[i + 1, j], 1.0, gram[i, j + 1])
            add_into(gram[i + 1, j], (SHIFTS[j] - SHIFTS[i]) / SCALE_POWER, gram[i, j])
    image = {}
    for i in range(DEPTH):
        for j in range(DEPTH):
            image[i, j] = {}
            for a, left in ((i, SHIFTS[i]), (i + 1, SCALE_POWER)):
                for b, right in ((j, SHIFTS[j]), (j + 1, SCALE_POWER)):
                    add_into(image[i, j], left * right, gram[a, b])
    for i in range(DEPTH):
        image[i, DEPTH] = image[DEPTH, i] = {i: SHIFTS[i], i + 1: SCALE_POWER}
    return gram, image


def assemble(shifted, table, size):
    _, lane = iotas()
    block = lane // NRHS
    tiles = []
    for i in range(size):
        total = jnp.zeros(TILE, jnp.float32)
        places = [(j, k, value) for j in range(size) for k, value in table.get((i, j), {}).items() if value]
        for d in sorted({k - j for j, k, _ in places}):
            factor = jnp.zeros(TILE, jnp.float32)
            for j, k, value in places:
                if k - j == d:
                    factor = jnp.where(block == j, value, factor)
            total = total + factor * shifted[d]
        tiles.append(total)
    return tiles


def plus_transpose(tiles):
    whole = jnp.concatenate(tiles + [jnp.zeros((LANES - 8 * len(tiles), LANES), jnp.float32)], 0)
    turned = jnp.transpose(whole)
    return [t + turned[8 * b : 8 * b + 8] for b, t in enumerate(tiles)]


def lane_of(tile, index):
    return jnp.broadcast_to(tile[:, index : index + 1], TILE)


def row_of(tile, index):
    return jnp.broadcast_to(tile[index : index + 1, :], TILE)


def eliminate(tiles):
    row, _ = iotas()
    tiles = list(tiles)
    for p in range(DEPTH):
        columns = [[lane_of(t, NRHS * p + c) for t in tiles] for c in range(NRHS)]
        for c in range(NRHS):
            pivot = 1.0 / row_of(columns[c][p], c)
            factor = [t * pivot for t in columns[c]]

            def step(rows):
                pivot_row = row_of(rows[p], c)
                out = [t - f * pivot_row for t, f in zip(rows, factor)]
                out[p] = jnp.where(row == c, pivot_row * pivot, out[p])
                return out

            for later in range(c + 1, NRHS):
                columns[later] = step(columns[later])
            tiles = step(tiles)
    return tiles


def combine_kernel(total, basis, correction, new_residual, estimate, weights, results, sem):
    row, lane = iotas()
    words = total[...]
    low = jnp.where(lane < 56, pltpu.roll(words, 56, 1), pltpu.roll(words, 116, 1))
    moments = jnp.where(row < 4, words, pltpu.roll(low, 4, 0))
    place = lane % NRHS
    half = jnp.where(row == place, 0.5, 1.0)
    moments = jnp.where((row <= place) & (lane < MOMENTS * NRHS), half * moments, 0.0)
    shifted = {d: pltpu.roll(moments, -NRHS * d % LANES, 1) for d in range(-DEPTH, MOMENTS)}
    gram_table, image_table = expansions()
    tiles = plus_transpose(assemble(shifted, image_table, BLOCKS))[:DEPTH]
    coeffs = eliminate(tiles)
    first = NRHS * DEPTH
    inside = (lane >= first) & (lane < first + NRHS)
    unit = jnp.where(lane == row + first, 1.0, 0.0)
    kept = []
    for j in range(BLOCKS):
        value = unit if j == 0 else jnp.zeros(TILE, jnp.float32)
        if j < DEPTH:
            value = value - SHIFTS[j] * coeffs[j]
        if j:
            value = value - SCALE_POWER * coeffs[j - 1]
        kept.append(jnp.where(inside, value, 0.0))
    for r in range(NRHS):
        for k, tile in enumerate(coeffs + kept):
            weights[r, k] = lane_of(tile, first + r)

    gram = plus_transpose(assemble(shifted, gram_table, BLOCKS))
    size = BLOCKS * NRHS
    side = jnp.concatenate(kept, 0)
    product = jnp.dot(
        jnp.concatenate(gram, 0)[:, :size], side, precision=lax.Precision.HIGHEST, preferred_element_type=jnp.float32
    )
    left_over = jnp.sum(side * product, axis=0, keepdims=True)
    start = jnp.sum(jnp.where(row == lane, gram[0], 0.0), axis=0, keepdims=True)
    estimate[...] = left_over[:, first : first + NRHS] / start[:, :NRHS]

    spots = [(plane_x, h) for plane_x in range(DEPTH) for h in (0, 1)]

    def at(ref, spot, *index):
        plane_x, h = spot
        return ref.at[(*index, plane_x, slice(None), pl.ds(h * LANES, LANES))]

    def field(r, _):
        sums = [[jnp.zeros(TILE, jnp.float32)] * len(spots) for _ in range(2)]
        for j in range(BLOCKS):
            for e in range(NRHS):
                values = [at(basis, spot, j, e)[...] for spot in spots]
                for n in (0, 1):
                    if n == 0 and j == DEPTH:
                        continue
                    factor = jnp.broadcast_to(weights[r, n * DEPTH + j, e : e + 1, :], TILE)
                    sums[n] = [s + factor * v for s, v in zip(sums[n], values)]
        for n, out in enumerate((correction, new_residual)):
            for spot, s in zip(spots, sums[n]):
                at(results, spot, n, r)[...] = s
            pltpu.make_async_copy(results.at[n, r], out.at[r], sem).start()
        return 0

    lax.fori_loop(0, NRHS, field, 0)
    pltpu.make_async_copy(results, results, sem).wait()


def solution(mesh, plane_sides=PLANE_SIDES):
    ny, nx = plane_sides
    sides = (mesh.shape["gx"] // ny, ny, nx)
    vmem, hbm = pl.BlockSpec(memory_space=pltpu.VMEM), pl.BlockSpec(memory_space=pltpu.HBM)
    f32 = jnp.float32

    def body(residual, diagonal):
        cells = residual.shape[1:]
        extended = (NRHS + 1, SPAN, *cells[1:])
        dma = pltpu.SemaphoreType.DMA
        basis, total = pl.pallas_call(
            functools.partial(moments_kernel, sides),
            name="moments",
            out_shape=(
                jax.ShapeDtypeStruct((BLOCKS, *residual.shape), f32),
                jax.ShapeDtypeStruct(TILE, f32),
            ),
            in_specs=[hbm, hbm],
            out_specs=(vmem, vmem),
            scratch_shapes=[
                pltpu.VMEM(extended, f32),
                pltpu.VMEM(extended, f32),
                pltpu.VMEM((DEPTH, SPAN, 4, *TILE), f32),
                pltpu.VMEM(TILE, f32),
                pltpu.VMEM((ny * nx * 2 - 1, ROWS, LANES), f32),
                pltpu.VMEM((sides[0] - 1, ROWS, LANES), f32),
                pltpu.VMEM((ROWS, LANES), f32),
                dma((NRHS + 1,)),
                dma((NRHS + 1,)),
                dma((NRHS + 1,)),
                dma,
                dma,
                dma,
                dma,
                dma,
                dma,
                pltpu.SemaphoreType.REGULAR((4,)),
            ],
            compiler_params=pltpu.CompilerParams(collective_id=0, has_side_effects=True, vmem_limit_bytes=VMEM_BYTES),
        )(residual, diagonal)
        correction, new_residual, estimate = pl.pallas_call(
            combine_kernel,
            name="combine",
            out_shape=(
                jax.ShapeDtypeStruct(residual.shape, f32),
                jax.ShapeDtypeStruct(residual.shape, f32),
                jax.ShapeDtypeStruct((1, NRHS), f32),
            ),
            in_specs=[vmem, vmem],
            out_specs=(hbm, hbm, vmem),
            scratch_shapes=[
                pltpu.VMEM((NRHS, DEPTH + BLOCKS, *TILE), f32),
                pltpu.VMEM((2, *residual.shape), f32),
                dma,
            ],
            compiler_params=pltpu.CompilerParams(vmem_limit_bytes=VMEM_BYTES),
        )(total, basis)
        return correction, new_residual, estimate.reshape(NRHS)

    placed = P(None, "gx", "gy", None)
    return jax.shard_map(
        body,
        mesh=mesh,
        in_specs=(placed, P("gx", "gy", None)),
        out_specs=(placed, placed, P()),
        check_vma=False,
    )
```

time: 205 us -> 63.1 us (0.31)
  the two profiles are of different devices: /device:TPU:2 before, /device:TPU:1 now
where the time goes in v2:
time: 63.1 us; the launch traced here: 62.1 us
  Pallas kernels  59.8 us (95%)
  local copies, waits for them, and re-layouts  1.7 us (3%)
  between operations  0.65 us (1%)
    pallas_call x1, Pallas kernels, body(): pl.pallas_call(functools.partial(moments_kernel, sides), name='moments',...  55.5 us
    pallas_call x1, Pallas kernels, body(): pl.pallas_call(combine_kernel, name='combine', out_shape=(jax.ShapeDtypeS...  4.23 us
    unnamed x4, local copies, waits for them, and re-layouts  1.7 us

profile of v2, /device:TPU:1, one launch (start us, length us, event | category | flops | bytes accessed | tf_op | source)
XLA Modules:
  0.0 62.1 jit_solution(4404423591212505163)
XLA Ops:
  0.6 0.0 copy-start
  0.6 0.9 %copy-done = f32[8,4,8,256]{3,2,1,0:T(8,128)S(1)} copy-done((f32[8,4,8,256]{3,2,1,0:T(8,128)S(1)}, f32[8,4,8,256]{3,2,1,0:T(8,128)}, u32[]{:S(2)}) %copy-start) | copy-done | bytes 262168
  1.6 0.0 copy-start.1
  1.6 0.8 %copy-done.1 = f32[4,8,256]{2,1,0:T(8,128)S(1)} copy-done((f32[4,8,256]{2,1,0:T(8,128)S(1)}, f32[4,8,256]{2,1,0:T(8,128)}, u32[]{:S(2)}) %copy-start.1) | copy-done | bytes 32792
  2.3 55.5 %moments.1 = (f32[5,8,4,8,256]{4,3,2,1,0:T(8,128)S(1)}, f32[8,128]{1,0:T(8,128)S(1)}) custom-call(f32[8,4,8,256]{3,2,1,0:T(8,128)S(1)} %copy-done, f32[4,8,256]{2,1,0:T(8,128)S(1)} %copy-done.1), custom_call_target="tpu_custom_call" | custom-call | tf_op jit(solution)/shard_map/moments/pallas_call | solution.py:447
  57.9 4.2 %combine.1 = (f32[8,4,8,256]{3,2,1,0:T(8,128)}, f32[8,4,8,256]{3,2,1,0:T(8,128)}, f32[1,8]{1,0:T(1,128)}) custom-call(f32[8,128]{1,0:T(8,128)S(1)} %get-tuple-element.8.total, f32[5,8,4,8,256]{4,3,2,1,0:T(8,128)S(1)} %get-tuple-element.9.basis), custom_call_target="tpu_custom_call" | custom-call | tf_op jit(solution)/shard_map/combine/pallas_call | solution.py:477
Async XLA Ops:
  0.6 1.0 %copy-start = (f32[8,4,8,256]{3,2,1,0:T(8,128)S(1)}, f32[8,4,8,256]{3,2,1,0:T(8,128)}, u32[]{:S(2)}) copy-start(f32[8,4,8,256]{3,2,1,0:T(8,128)} %residual.1) | copy-start | bytes 786436
  1.6 0.8 %copy-start.1 = (f32[4,8,256]{2,1,0:T(8,128)S(1)}, f32[4,8,256]{2,1,0:T(8,128)}, u32[]{:S(2)}) copy-start(f32[4,8,256]{2,1,0:T(8,128)} %diagonal.1) | copy-start | bytes 98308
